TPU v7x, 32 devices: a whole 2x2x4 slice. The times are simulated.
32 devices in a mesh: band: 8 (over y, x, core), ga: 4 (over z).
Axes of the slice: x: 2, y: 2, z: 4, core: 2. Of those that a mesh axis runs over, the one named last changes fastest.
Arguments:
- orbitals: bfloat16 [256, 90112], P(('band', 'ga')), may hold values from -6 to 6
- local_part: bfloat16 [256, 90112], P(('band', 'ga')), may hold values from -6 to 6
- projectors: bfloat16 [90112, 1664], P(('band', 'ga')), may hold values from -0.01953125 to 0.01953125
- couplings: float32 [4, 13, 13], replicated, may hold values from -20 to 20, as said below
- species: int32 [128], replicated, may hold values from 0 to 3
Outputs:
- applied: bfloat16 [256, 90112], P(('band', 'ga'))
Inputs may be any that keep to these rules, and one draw needn't show every extreme that they name: `couplings`: each species has one symmetric block.
All inputs are finite; a program needn't handle non-finite values.
Results may differ from a plain program's by a relative error of at most 0.0056.
Values may be sent and summed in bfloat16 or wider, within the bound.
A program may use at most 64 MiB of HBM per device.

v0:
```python
import jax
import jax.numpy as jnp
from jax import lax
from jax.sharding import PartitionSpec as P


def select_blocks(couplings, species):
    kinds = couplings.shape[0]
    width = couplings.shape[1]
    select = (jnp.arange(kinds, dtype=jnp.int32)[:, None] == species[None, :]).astype(jnp.float32)
    table = jnp.einsum(
        "sk,sa->ka",
        couplings.reshape(kinds, width * width),
        select,
        precision=lax.Precision.HIGHEST,
    )
    return table.reshape(width, width, species.shape[0])


def couple(totals, blocks):
    width = blocks.shape[0]
    atom_count = blocks.shape[2]
    folded = totals.reshape(totals.shape[0], width, atom_count)
    mixed = jnp.zeros_like(folded)
    for inner in range(width):
        mixed = mixed + folded[:, inner, None, :] * blocks[None, inner, :, :]
    return mixed.reshape(totals.shape[0], width * atom_count).astype(jnp.bfloat16)


def expand(coefs, projectors):
    return jnp.einsum("bp,gp->bg", coefs, projectors, preferred_element_type=jnp.float32).astype(
        jnp.bfloat16
    )


def on_device(orbitals, local_part, projectors, couplings, species):
    blocks = select_blocks(couplings, species)
    slab_orbitals = lax.all_to_all(
        orbitals, ("band", "ga"), split_axis=1, concat_axis=0, tiled=True
    )
    partial_value = jnp.dot(slab_orbitals, projectors, preferred_element_type=jnp.float32)
    totals = lax.psum(partial_value, ("band", "ga"))
    slab_correction = expand(couple(totals, blocks), projectors)
    correction = lax.all_to_all(
        slab_correction, ("band", "ga"), split_axis=0, concat_axis=1, tiled=True
    )
    correction = lax.optimization_barrier(correction)
    return (local_part.astype(jnp.float32) + correction.astype(jnp.float32)).astype(jnp.bfloat16)


def solution(mesh):
    placed = (P(("band", "ga"), None), P(("band", "ga"), None), P(("band", "ga"), None), P(), P())
    return jax.shard_map(
        on_device, mesh=mesh, in_specs=placed, out_specs=P(("band", "ga"), None), check_vma=False
    )
```

profile of v0, /device:TPU:1, one launch (start us, length us, event | category | flops | bytes accessed | tf_op | source)
XLA Modules:
  0.0 247.2 jit_solution(7646724141969409436)
XLA Ops:
  6.5 0.0 all-reduce.2.cloned.1.call-start
  6.5 42.4 %all_to_all.38 = bf16[8,32,2816]{2,0,1:T(8,128)(2,1)S(1)} all-to-all(bf16[8,32,2816]{2,0,1:T(8,128)(2,1)} %bitcast.148), channel_id=1, replica_groups=mesh['band'=8,'ga'=4] {'band','ga'}, dimensions={1} | all-to-all | bytes 2883584 | tf_op jit(solution)/shard_map/all_to_all | solution.py:38
  48.9 8.6 %fusion.14 = f32[256,1664]{0,1:T(8,128)} fusion(bf16[2816,1664]{1,0:T(8,128)(2,1)} %param.7, bf16[8,32,2816]{2,0,1:T(8,128)(2,1)S(1)} %all_to_all.38), kind=kOutput, calls=%fused_computation.29 | convolution fusion | flops 2399141888 | bytes 12517376 | tf_op jit(solution)/shard_map/dot_general | solution.py:41
  57.5 0.0 copy-start.1
  57.5 0.0 copy-start.2
  57.5 0.0 all-reduce.2.cloned.1.call-update
  57.6 0.7 copy-done.1
  58.3 0.1 reshape.81
  58.4 0.0 copy-done.2
  58.4 0.3 convolution_bitcast_fusion
  58.7 129.1 %all-reduce.2.cloned.1.call-done = f32[256,13,128]{0,2,1:T(8,128)} async-done(((f32[256,13,128]{0,2,1:T(8,128)}), f32[256,13,128]{0,2,1:T(8,128)}) %all-reduce.2.cloned.1.call-update) | async-done | bytes 1703952 | tf_op jit(solution)/shard_map/psum | solution.py:42
  187.8 1.6 slice_bitcast_fusion.12
  189.3 3.0 %fusion.2 = bf16[256,1664]{0,1:T(8,128)(2,1)S(1)} fusion(f32[1664]{0:T(1024)S(1)} %get-tuple-element.19, f32[256,128]{0,1:T(8,128)S(1)} %get-tuple-element.6, f32[1664]{0:T(1024)S(1)} %get-tuple-element.20, f32[256,128]{0,1:T(8,128)S(1)} %get-tuple-element.7, f32[1664]{0:T(1024)S(1)} %get-tuple-element.21, f32[256,128]{0,1:T(8,128)S(1)} %get-tuple-element.8, ...), kind=kLoop, calls=%fused_computation.5 | loop fusion | flops 11075584 | bytes 2642432 | tf_op jit(solution)/shard_map/convert_element_type | solution.py:27
  192.3 6.6 %fusion = bf16[32,8,2816]{2,1,0:T(8,128)(2,1)S(1)} fusion(bf16[256,1664]{0,1:T(8,128)(2,1)S(1)} %fusion.2, bf16[2816,1664]{1,0:T(8,128)(2,1)} %param.7), kind=kOutput, calls=%fused_computation.1 | convolution fusion | flops 2399862784 | bytes 11665408 | tf_op jit(solution)/shard_map/bp,gp->bg/dot_general | solution.py:31
  198.9 0.0 copy-start
  198.9 40.0 %all_to_all.39 = bf16[32,8,2816]{2,1,0:T(8,128)(2,1)S(1)} all-to-all(bf16[32,8,2816]{2,1,0:T(8,128)(2,1)S(1)} %fusion), channel_id=1, replica_groups=mesh['band'=8,'ga'=4] {'band','ga'}, dimensions={0} | all-to-all | bytes 2883584 | tf_op jit(solution)/shard_map/all_to_all | solution.py:44
  238.9 0.0 copy-done
  238.9 1.4 add_convert_fusion
  (2 shorter events, 0.0 us)
Async XLA Ops:
  6.5 181.2 %all-reduce.2.cloned.1.call-start = ((), (), s32[]{:S(2)}) async-start(), calls=%async_computation.2 | async-start | bytes 3407872 | tf_op jit(solution)/shard_map/psum | solution.py:42
  57.5 0.7 copy-start.1
  57.5 0.8 copy-start.2
  198.9 40.0 %copy-start = (bf16[8,90112]{1,0:T(8,128)(2,1)S(1)}, bf16[8,90112]{1,0:T(8,128)(2,1)}, u32[]{:S(2)}) copy-start(bf16[8,90112]{1,0:T(8,128)(2,1)} %param.6) | copy-start | bytes 4325380
Sparse Core Ops, SparseCore 0:
  57.7 130.0 all-reduce.1
where the time goes:
time: 248 us; the launch traced here: 247 us
  waiting for transfers between devices  129 us (52%)
  blocking collectives  82.4 us (33%)
  matrix products  15.5 us (6%)
  between operations  13.4 us (5%)
  other arithmetic  4.41 us (2%)
    psum x1, waiting for transfers between devices, on_device(): totals = lax.psum(partial_value, ('band', 'ga'))  129 us
    all_to_all x1, blocking collectives, on_device(): lax.all_to_all(orbitals, ('band', 'ga'), split_axis=1, concat_axis=0, til...  42.4 us
    all_to_all x1, blocking collectives, on_device(): lax.all_to_all(slab_correction, ('band', 'ga'), split_axis=0, concat_axis...  40 us
    dot_general x1, matrix products, on_device(): jnp.dot(slab_orbitals, projectors, preferred_element_type=jnp.float32)  8.63 us
    dot_general x1, matrix products, expand(): jnp.einsum('bp,gp->bg', coefs, projectors, preferred_element_type=jnp.flo...  6.58 us
  transfers between devices with their start and end apart: 1, of which 1 were waited for; matrix products, arithmetic and copies ran while one was open for 0% of the time, Pallas kernels for 0%

commit v1 on v0

--- a/solution.py
+++ b/solution.py
@@ -39,7 +39,7 @@
         orbitals, ("band", "ga"), split_axis=1, concat_axis=0, tiled=True
     )
     partial_value = jnp.dot(slab_orbitals, projectors, preferred_element_type=jnp.float32)
-    totals = lax.psum(partial_value, ("band", "ga"))
+    totals = lax.psum(lax.psum(partial_value, "ga"), "band")
     slab_correction = expand(couple(totals, blocks), projectors)
     correction = lax.all_to_all(
         slab_correction, ("band", "ga"), split_axis=0, concat_axis=1, tiled=True

time: 248 us -> 249 us (level)
  local copies, waits for them, and re-layouts: 2.42 us -> 5.14 us
    psum x0 -> x1, local copies, waits for them, and re-layouts: none -> 2.73 us  [on_device(): totals = lax.psum(lax.psum(partial_value, 'ga'), 'band')]
    psum x1 -> x2, waiting for transfers between devices: 129 us -> 128 us  [on_device(): totals = lax.psum(lax.psum(partial_value, 'ga'), 'band')]
  transfers between devices with their start and end apart: 1 -> 2, of which waited for: 1 -> 2; matrix products, arithmetic and copies ran while one was open for 0% -> 0% of each run, Pallas kernels for 0% -> 0%
where the time goes in v1:
time: 249 us; the launch traced here: 248 us
  waiting for transfers between devices  128 us (51%)
  blocking collectives  82.7 us (33%)
  matrix products  14.5 us (6%)
  between operations  13.5 us (5%)
  local copies, waits for them, and re-layouts  5.14 us (2%)
  other arithmetic  4.41 us (2%)
    psum x2, waiting for transfers between devices, on_device(): totals = lax.psum(lax.psum(partial_value, 'ga'), 'band')  128 us
    all_to_all x1, blocking collectives, on_device(): lax.all_to_all(orbitals, ('band', 'ga'), split_axis=1, concat_axis=0, til...  42.4 us
    all_to_all x1, blocking collectives, on_device(): lax.all_to_all(slab_correction, ('band', 'ga'), split_axis=0, concat_axis...  40.4 us
    dot_general x1, matrix products, on_device(): jnp.dot(slab_orbitals, projectors, preferred_element_type=jnp.float32)  7.69 us
    dot_general x1, matrix products, expand(): jnp.einsum('bp,gp->bg', coefs, projectors, preferred_element_type=jnp.flo...  6.58 us
  transfers between devices with their start and end apart: 2, of which 2 were waited for; matrix products, arithmetic and copies ran while one was open for 0% of the time, Pallas kernels for 0%

profile of v1, /device:TPU:1, one launch (start us, length us, event | category | flops | bytes accessed | tf_op | source)
XLA Modules:
  0.0 248.5 jit_solution(16487304538324887462)
XLA Ops:
  6.5 0.0 all-reduce.3.cloned.1.call-start
  6.5 42.4 %all_to_all.38 = bf16[8,32,2816]{2,0,1:T(8,128)(2,1)S(1)} all-to-all(bf16[8,32,2816]{2,0,1:T(8,128)(2,1)} %bitcast.148), channel_id=1, replica_groups=mesh['band'=8,'ga'=4] {'band','ga'}, dimensions={1} | all-to-all | bytes 2883584 | tf_op jit(solution)/shard_map/all_to_all | solution.py:38
  48.9 7.7 %fusion.14 = f32[256,1664]{1,0:T(8,128)} fusion(bf16[2816,1664]{1,0:T(8,128)(2,1)} %param.7, bf16[8,32,2816]{2,0,1:T(8,128)(2,1)S(1)} %all_to_all.38), kind=kOutput, calls=%fused_computation.29 | convolution fusion | flops 2399141888 | bytes 12517376 | tf_op jit(solution)/shard_map/dot_general | solution.py:41
  56.6 0.0 all-reduce.3.cloned.1.call-update
  56.6 0.0 all-reduce.5.cloned.1.call-start
  56.7 70.2 %all-reduce.3.cloned.1.call-done = f32[256,1664]{1,0:T(8,128)} async-done(((f32[256,1664]{1,0:T(8,128)}), f32[256,1664]{1,0:T(8,128)}) %all-reduce.3.cloned.1.call-update) | async-done | bytes 1703952 | tf_op jit(solution)/shard_map/psum | solution.py:42
  126.9 2.7 %copy.6 = f32[256,1664]{0,1:T(8,128)} copy(f32[256,1664]{1,0:T(8,128)} %all-reduce.3.cloned.1.call-done) | data formatting | bytes 3407872 | tf_op jit(solution)/shard_map/psum | solution.py:42
  129.6 0.0 copy-start.1
  129.6 0.0 copy-start.2
  129.6 0.0 all-reduce.5.cloned.1.call-update
  129.6 0.7 copy-done.1
  130.4 0.1 reshape.81
  130.4 0.0 copy-done.2
  130.5 0.3 convolution_bitcast_fusion
  130.7 57.9 %all-reduce.5.cloned.1.call-done = f32[256,13,128]{0,2,1:T(8,128)} async-done(((f32[256,13,128]{0,2,1:T(8,128)}), f32[256,13,128]{0,2,1:T(8,128)}) %all-reduce.5.cloned.1.call-update) | async-done | bytes 1703952 | tf_op jit(solution)/shard_map/psum | solution.py:42
  188.7 1.6 slice_bitcast_fusion.12
  190.3 3.0 %fusion.2 = bf16[256,1664]{0,1:T(8,128)(2,1)S(1)} fusion(f32[1664]{0:T(1024)S(1)} %get-tuple-element.19, f32[256,128]{0,1:T(8,128)S(1)} %get-tuple-element.6, f32[1664]{0:T(1024)S(1)} %get-tuple-element.20, f32[256,128]{0,1:T(8,128)S(1)} %get-tuple-element.7, f32[1664]{0:T(1024)S(1)} %get-tuple-element.21, f32[256,128]{0,1:T(8,128)S(1)} %get-tuple-element.8, ...), kind=kLoop, calls=%fused_computation.5 | loop fusion | flops 11075584 | bytes 2642432 | tf_op jit(solution)/shard_map/convert_element_type | solution.py:27
  193.3 6.6 %fusion = bf16[32,8,2816]{2,1,0:T(8,128)(2,1)S(1)} fusion(bf16[256,1664]{0,1:T(8,128)(2,1)S(1)} %fusion.2, bf16[2816,1664]{1,0:T(8,128)(2,1)} %param.7), kind=kOutput, calls=%fused_computation.1 | convolution fusion | flops 2399862784 | bytes 11665408 | tf_op jit(solution)/shard_map/bp,gp->bg/dot_general | solution.py:31
  199.8 0.0 copy-start
  199.9 40.4 %all_to_all.39 = bf16[32,8,2816]{2,1,0:T(8,128)(2,1)S(1)} all-to-all(bf16[32,8,2816]{2,1,0:T(8,128)(2,1)S(1)} %fusion), channel_id=1, replica_groups=mesh['band'=8,'ga'=4] {'band','ga'}, dimensions={0} | all-to-all | bytes 2883584 | tf_op jit(solution)/shard_map/all_to_all | solution.py:44
  240.2 0.0 copy-done
  240.2 1.4 add_convert_fusion
  (2 shorter events, 0.0 us)
Async XLA Ops:
  6.5 120.3 %all-reduce.3.cloned.1.call-start = ((), (), s32[]{:S(2)}) async-start(), calls=%async_computation.2 | async-start | bytes 3407872 | tf_op jit(solution)/shard_map/psum | solution.py:42
  56.6 132.1 %all-reduce.5.cloned.1.call-start = ((), (), s32[]{:S(2)}) async-start(), calls=%async_computation.3 | async-start | bytes 3407872 | tf_op jit(solution)/shard_map/psum | solution.py:42
  129.6 0.7 copy-start.1
  129.6 0.8 copy-start.2
  199.8 40.4 %copy-start = (bf16[8,90112]{1,0:T(8,128)(2,1)S(1)}, bf16[8,90112]{1,0:T(8,128)(2,1)}, u32[]{:S(2)}) copy-start(bf16[8,90112]{1,0:T(8,128)(2,1)} %param.6) | copy-start | bytes 4325380
Sparse Core Ops, SparseCore 0:
  56.7 70.0 all-reduce.2
  130.1 58.4 all-reduce.4
